TPU v7x, 256 devices: a 2x2x32 block of a 4x8x32 slice. The times are simulated.
256 devices in a mesh: groups: 4 (over x, y), patch: 64 (over z, core).
Axes of the slice: x: 2, y: 2, z: 32, core: 2. Of those that a mesh axis runs over, the one named last changes fastest.
The devices are a block of a 4x8x32 slice.
Arguments:
- tokens: bfloat16 [131072, 1152], P(('groups', 'patch')), parts along dimension 0, may hold values from -6 to 6
- stale_kv: bfloat16 [131072, 1152], P(('groups', 'patch')), parts along dimension 0, may hold values from -40 to 40, as said below
- mod_table: float32 [6, 1152], replicated, may hold values from -2 to 3
- mod_mix: float32 [6, 1152], replicated, may hold values from -3 to 3
- timestep: int32 [4], P('groups'), parts along dimension 0, may hold values from 0 to 999
- frame_order: int32 [64], P('groups'), parts along dimension 0, may hold values from 0 to 15, each once
- spatial_qkv: bfloat16 [3, 1152, 576], replicated, may hold values from -0.1875 to 0.1875
- spatial_out: bfloat16 [576, 1152], replicated, may hold values from -0.25 to 0.25
- temporal_qkv: bfloat16 [3, 1152, 576], replicated, may hold values from -0.1875 to 0.1875
- temporal_out: bfloat16 [576, 1152], replicated, may hold values from -0.25 to 0.25
Outputs:
- block_out: float32 [131072, 1152], P(('groups', 'patch')), parts along dimension 0
There are 4 independent parts, one for each index of `groups`. A program takes and returns all parts, laid end to end along the dimension named above; an argument that names none is the same for every part. Nothing has to cross between parts.
Inputs may be any that keep to these rules, and one draw needn't show every extreme that they name: `frame_order`: a permutation of the 16 time positions. `stale_kv`: previous step's keys and values.
All inputs are finite; a program needn't handle non-finite values.
Results may differ from a plain program's by a relative error of at most 0.013.
The roundings to bfloat16 on the way count: a program that leaves them out, or rounds other values in their place, can miss the bound.
Values may be sent and summed in bfloat16 or wider, within the bound.
A program may use at most 128 MiB of HBM per device.

v0:
```python
import math

import jax
import jax.numpy as jnp
from jax import lax
from jax.sharding import Mesh
from jax.sharding import PartitionSpec as P

HEADS = 16
PATCH = ("patch_0", "patch_1")
GROUPS_PATCH = ("groups", "patch_0", "patch_1")


epsilon = 1e-06


def from_partner(value, axis, distance):
    mask = 2**distance
    pairs = [(source, source ^ mask) for source in range(lax.axis_size(axis))]
    return lax.ppermute(value, axis, pairs)


def split_up(value, dim, count):
    lengths = value.shape
    parts = value.reshape(*lengths[:dim], count, lengths[dim] // count, *lengths[dim + 1 :])
    return jnp.moveaxis(parts, dim, 0)


def in_order(parts, dim):
    parts = jnp.moveaxis(parts, 0, dim)
    lengths = parts.shape
    return parts.reshape(*lengths[:dim], lengths[dim] * lengths[dim + 1], *lengths[dim + 2 :])


def moved_by_axis(parts, axes, turns):
    lengths = [lax.axis_size(a) for a in axes]
    parts = parts.reshape(*lengths, *parts.shape[1:])
    for k in turns:
        parts = lax.all_to_all(parts, axes[k], split_axis=k, concat_axis=k, tiled=True)
    return parts.reshape(-1, *parts.shape[len(axes) :])


def two_step_exchange(value, groups, turns, split_dim, concat_dim):
    count = lax.axis_size(groups[0]) * lax.axis_size(groups[1])
    parts = split_up(value, split_dim, count)
    return in_order(moved_by_axis(parts, groups, turns), concat_dim)


def normalize(activations):
    row_mean = jnp.mean(activations, axis=-1, keepdims=True)
    centered = activations - row_mean
    variance = jnp.mean(centered * centered, axis=-1, keepdims=True)
    return centered * lax.rsqrt(variance + epsilon)


def sinusoid(position, feature_width):
    half_width = feature_width // 2
    frequencies = jnp.exp(
        -math.log(10000.0) * jnp.arange(half_width, dtype=jnp.float32) / half_width
    )
    angles = jnp.asarray(position).astype(jnp.float32)[..., None] * frequencies
    return jnp.concatenate([jnp.sin(angles), jnp.cos(angles)], axis=-1)


def softmax_rows(scores):
    row_top = jnp.max(scores, axis=-1, keepdims=True)
    exp_scores = jnp.exp(scores - row_top)
    return (exp_scores / jnp.sum(exp_scores, axis=-1, keepdims=True)).astype(jnp.bfloat16)


def spatial_attend(queries, key_rows, value_rows, head_dim):
    width_win = queries.shape[1]
    head_count = width_win // head_dim
    query_heads = queries.reshape(-1, head_count, head_dim)
    key_heads = key_rows.reshape(-1, head_count, head_dim)
    value_heads = value_rows.reshape(-1, head_count, head_dim)
    scores = jnp.einsum(
        "qhe,khe->hqk", query_heads, key_heads, preferred_element_type=jnp.float32
    ) * head_dim ** (-0.5)
    weights = softmax_rows(scores)
    mixed_out = jnp.einsum("hqk,khe->qhe", weights, value_heads, preferred_element_type=jnp.float32)
    return mixed_out.reshape(-1, width_win).astype(jnp.bfloat16)


def temporal_attend(queries, key_rows, value_rows, head_dim):
    frame_count, pixel_count, width_win = queries.shape
    head_count = width_win // head_dim
    shape_heads = (frame_count, pixel_count, head_count, head_dim)
    query_heads = queries.reshape(shape_heads)
    key_heads = key_rows.reshape(shape_heads)
    value_heads = value_rows.reshape(shape_heads)
    scores = jnp.einsum(
        "fmhe,gmhe->mhfg", query_heads, key_heads, preferred_element_type=jnp.float32
    ) * head_dim ** (-0.5)
    weights = softmax_rows(scores)
    mixed_out = jnp.einsum(
        "mhfg,gmhe->fmhe", weights, value_heads, preferred_element_type=jnp.float32
    )
    return mixed_out.reshape(frame_count, pixel_count, width_win).astype(jnp.bfloat16)


def per_device(
    tokens,
    stale_kv,
    mod_table,
    mod_mix,
    timestep,
    frame_order,
    spatial_qkv,
    spatial_out,
    temporal_qkv,
    temporal_out,
):
    devices = lax.axis_size(PATCH)
    dev_index = lax.axis_index(PATCH)
    frames = devices // 4
    quarter = dev_index % 4
    frame_slot = dev_index // 4
    row_count, feature_width = tokens.shape
    width_win = spatial_out.shape[0]
    head_dim = feature_width // HEADS
    modulation = mod_table + mod_mix * sinusoid(timestep[0], feature_width)[None, :]
    tokens_wide = tokens.astype(jnp.float32)
    spatial_in = (normalize(tokens_wide) * (1.0 + modulation[1]) + modulation[0]).astype(
        jnp.bfloat16
    )
    fresh_qkv = jnp.einsum(
        "tr,jrd->jtd", spatial_in, spatial_qkv, preferred_element_type=jnp.float32
    ).astype(jnp.bfloat16)
    bit_order = (0, 1)
    kv_block = stale_kv
    for bit_num in bit_order:
        partner = from_partner(kv_block, PATCH, bit_num)
        low_half = dev_index >> bit_num & 1 == 0
        kv_block = jnp.where(
            low_half, jnp.stack([kv_block, partner], 0), jnp.stack([partner, kv_block], 0)
        )
    kv_block = kv_block.reshape(4, row_count, 2 * width_win)
    own_mask = (jnp.arange(4) == quarter)[:, None, None]
    key_rows = jnp.where(own_mask, fresh_qkv[1][None], kv_block[:, :, :width_win]).reshape(
        4 * row_count, width_win
    )
    value_rows = jnp.where(own_mask, fresh_qkv[2][None], kv_block[:, :, width_win:]).reshape(
        4 * row_count, width_win
    )
    spatial_mixed = spatial_attend(fresh_qkv[0], key_rows, value_rows, head_dim)
    spatial_proj = jnp.dot(spatial_mixed, spatial_out, preferred_element_type=jnp.float32)
    after_spatial = tokens_wide + modulation[2] * spatial_proj
    frame_id = jnp.sum(jnp.where(jnp.arange(frames) == frame_slot, frame_order, 0))
    temporal_in = (
        normalize(after_spatial) * (1.0 + modulation[4])
        + modulation[3]
        + sinusoid(frame_id, feature_width)[None, :]
    ).astype(jnp.bfloat16)
    piece_rows = row_count // devices
    arriving = two_step_exchange(
        temporal_in.reshape(devices, piece_rows, feature_width),
        ("patch_0", "patch_1"),
        (1, 0),
        0,
        0,
    )
    arranged = arriving.reshape(frames, 4 * piece_rows, feature_width)
    flat_rows = arranged.reshape(-1, feature_width)
    temporal_proj = jnp.einsum(
        "tr,jrd->jtd", flat_rows, temporal_qkv, preferred_element_type=jnp.float32
    )
    temporal_proj = temporal_proj.astype(jnp.bfloat16).reshape(
        (3,) + arranged.shape[:-1] + (width_win,)
    )
    mixed_out = temporal_attend(temporal_proj[0], temporal_proj[1], temporal_proj[2], head_dim)
    returning = lax.all_to_all(
        mixed_out.reshape(devices, piece_rows, width_win),
        PATCH,
        split_axis=0,
        concat_axis=0,
        tiled=True,
    )
    temporal_mixed = returning.reshape(row_count, width_win)
    temporal_proj_out = jnp.dot(temporal_mixed, temporal_out, preferred_element_type=jnp.float32)
    return after_spatial + modulation[5] * temporal_proj_out


def solution(mesh):
    finer = Mesh(
        mesh.devices.reshape(mesh.shape["groups"], 32, 2), ("groups", "patch_0", "patch_1")
    )
    return jax.shard_map(
        per_device,
        mesh=finer,
        in_specs=(
            P(GROUPS_PATCH, None),
            P(GROUPS_PATCH, None),
            P(),
            P(),
            P("groups"),
            P("groups"),
            P(),
            P(),
            P(),
            P(),
        ),
        out_specs=P(GROUPS_PATCH, None),
        check_vma=False,
    )
```

profile of v0, /device:TPU:37, one launch (start us, length us, event | category | flops | bytes accessed | tf_op | source)
XLA Modules:
  0.0 386.7 jit_solution(15869654521814483930)
XLA Ops:
  0.0 20.4 %collective-permute-start = (bf16[512,1152]{1,0:T(8,128)(2,1)}, bf16[512,1152]{1,0:T(8,128)(2,1)S(1)}, u32[]{:S(2)}, u32[]{:S(2)}) collective-permute-start(bf16[512,1152]{1,0:T(8,128)(2,1)} %param.11), channel_id=1, source_target_pairs={{0,1},{1,0},{2,3},{3,2},{4,5},{5,4},{6,7},{7,6},{8,9},{9,8},{10,11... | collective-permute-start | bytes 3538952 | tf_op jit(solution)/shard_map/ppermute | solution.py:20
  21.2 1.5 convert_reduce_fusion
  23.5 3.9 maximum_select_fusion.2
  27.5 1.7 fusion.10
  29.2 5.2 %convert_bitcast_fusion.1 = bf16[3,512,576]{1,2,0:T(8,128)(2,1)S(1)} fusion(bf16[3,1152,576]{1,2,0:T(8,128)(2,1)} %param.16, bf16[512,1152]{1,0:T(8,128)(2,1)} %param.10, f32[1152]{0:T(1024)S(1)} %get-tuple-element.8, f32[1152]{0:T(1024)S(1)} %get-tuple-element.9, f32[512]{0:T(512)S(1)} %add_rsqrt_fusion.1, f32[512]{0:T(512)S(1)} %broadcast_multiply_fusion.1), kind=kOutput, calls=%fused_computation.33 | convolution fusion | flops 2042855424 | bytes 6943744 | tf_op jit(solution)/shard_map/tr,jrd->jtd/dot_general | solution.py:127
  34.4 1.3 slice_bitcast_fusion
  35.7 1.4 copy.33
  37.1 2.2 copy.31
  40.7 2.0 maximum_select_fusion.1
  42.7 37.7 %collective-permute-done.1 = bf16[2,512,1152]{2,1,0:T(8,128)(2,1)} collective-permute-done((bf16[2,512,1152]{2,1,0:T(8,128)(2,1)}, bf16[2,512,1152]{2,1,0:T(8,128)(2,1)}, u32[]{:S(2)}, u32[]{:S(2)}) %collective-permute-start.1) | collective-permute-done | bytes 2359328 | tf_op jit(solution)/shard_map/ppermute | solution.py:20
  80.4 3.1 maximum_select_fusion
  83.5 3.4 slice_select_fusion
  86.9 5.4 %copy.32 = bf16[4,512,576]{1,0,2:T(4,128)(2,1)} copy(bf16[4,512,576]{2,1,0:T(8,128)(2,1)} %get-tuple-element.12) | data formatting | bytes 4718592 | tf_op jit(solution)/shard_map/jit(_where)/select_n | solution.py:143
  92.3 5.8 %reshape_reshape.6 = bf16[2048,8,72]{0,2,1:T(8,128)(2,1)} reshape(bf16[4,512,576]{1,0,2:T(4,128)(2,1)} %copy.32) | data formatting | bytes 4718592 | tf_op jit(solution)/shard_map/reshape;reshape | solution.py:76
  98.2 5.4 %copy.34 = bf16[4,512,576]{1,0,2:T(4,128)(2,1)} copy(bf16[4,512,576]{2,1,0:T(8,128)(2,1)} %get-tuple-element.11) | data formatting | bytes 4718592 | tf_op jit(solution)/shard_map/jit(_where)/select_n | solution.py:140
  103.6 5.9 %reshape_reshape.7 = bf16[2048,8,72]{0,2,1:T(8,128)(2,1)} reshape(bf16[4,512,576]{1,0,2:T(4,128)(2,1)} %copy.34) | data formatting | bytes 4718592 | tf_op jit(solution)/shard_map/reshape;reshape | solution.py:75
  109.6 17.3 %fusion.56 = (f32[8,512]{1,0:T(8,128)S(1)}, f32[8,512,2048]{2,1,0:T(8,128)}) fusion(bf16[512,8,72]{0,2,1:T(8,128)(2,1)S(1)} %bitcast.55, bf16[2048,8,72]{0,2,1:T(8,128)(2,1)} %reshape_reshape.7), kind=kOutput, calls=%fused_computation.79 | convolution fusion | flops 1233127424 | bytes 36519936 | tf_op jit(solution)/shard_map/sub | solution.py:67
  126.8 14.1 %fusion.18 = bf16[8,72,512]{2,1,0:T(8,128)(2,1)S(1)} fusion(bf16[2048,8,72]{0,2,1:T(8,128)(2,1)} %reshape_reshape.6, f32[8,512,2048]{2,1,0:T(8,128)} %get-tuple-element.20, f32[8,512]{1,0:T(8,128)S(1)} %get-tuple-element.19), kind=kOutput, calls=%fused_computation.36 | convolution fusion | flops 1225031680 | bytes 36519936 | tf_op jit(solution)/shard_map/hqk,khe->qhe/dot_general | solution.py:81
  141.0 1.4 fusion.57
  143.9 5.3 %all_to_all.15 = bf16[32,2,1,8,1152]{4,3,0,2,1:T(8,128)(2,1)S(1)} all-to-all(bf16[32,2,1,8,1152]{4,3,0,2,1:T(8,128)(2,1)S(1)} %copy.35), channel_id=1, replica_groups=mesh['groups'=4,'patch_0'=32,'patch_1'=2] {'patch_1'}, dimensions={1} | all-to-all | bytes 2359296 | tf_op jit(solution)/shard_map/all_to_all | solution.py:39
  149.3 133.6 %all_to_all.16 = bf16[32,2,1,8,1152]{4,3,1,2,0:T(8,128)(2,1)S(1)} all-to-all(bf16[32,2,1,8,1152]{4,3,1,2,0:T(8,128)(2,1)S(1)} %copy.36), channel_id=1, replica_groups=mesh['groups'=4,'patch_0'=32,'patch_1'=2] {'patch_0'}, dimensions={0} | all-to-all | bytes 2359296 | tf_op jit(solution)/shard_map/all_to_all | solution.py:39
  282.9 2.5 convert_bitcast_fusion
  285.5 0.9 fusion.55
  286.4 1.4 copy.39
  287.7 2.0 reshape_squeeze.15
  290.0 2.0 reshape_squeeze.14
  292.3 1.0 reshape_squeeze.13
  293.4 4.8 %fusion.58 = (f32[32,8,16]{2,1,0:T(8,128)S(1)}, f32[32,8,16,16]{2,3,1,0:T(8,128)}) fusion(bf16[16,32,8,72]{3,2,1,0:T(8,128)(2,1)} %reshape_squeeze.15, bf16[16,32,8,72]{3,2,1,0:T(8,128)(2,1)} %reshape_squeeze.14), kind=kOutput, calls=%fused_computation.81 | convolution fusion | flops 9633807 | bytes 1458176 | tf_op jit(solution)/shard_map/sub | solution.py:67
  298.2 2.5 fusion.17
  300.9 0.8 convert_element_type.72
  301.8 80.3 %all_to_all.17 = bf16[64,8,576]{2,1,0:T(8,128)(2,1)S(1)} all-to-all(bf16[64,8,576]{2,1,0:T(8,128)(2,1)S(1)} %convert_element_type.72), channel_id=1, replica_groups=mesh['groups'=4,'patch_0'=32,'patch_1'=2] {'patch_0','patch_1'}, dimensions={0} | all-to-all | bytes 1179648 | tf_op jit(solution)/shard_map/all_to_all | solution.py:172
  382.1 4.7 %fusion.7 = f32[512,1152]{1,0:T(8,128)} fusion(f32[512,1152]{1,0:T(8,128)} %copy-done.1, bf16[576,1152]{1,0:T(8,128)(2,1)} %param.19, f32[1152]{0:T(1024)S(1)} %get-tuple-element.7, bf16[64,8,576]{2,1,0:T(8,128)(2,1)S(1)} %all_to_all.17), kind=kOutput, calls=%fused_computation.14 | convolution fusion | flops 680656896 | bytes 6640128 | tf_op jit(solution)/shard_map/dot_general | solution.py:180
  (39 shorter events, 4.3 us)
Async XLA Ops:
  0.0 141.0 %copy-start = (bf16[576,1152]{1,0:T(8,128)(2,1)S(1)}, bf16[576,1152]{1,0:T(8,128)(2,1)}, u32[]{:S(2)}) copy-start(bf16[576,1152]{1,0:T(8,128)(2,1)} %param.17) | copy-start | bytes 3981316
  0.0 23.5 %collective-permute-start = (bf16[512,1152]{1,0:T(8,128)(2,1)}, bf16[512,1152]{1,0:T(8,128)(2,1)S(1)}, u32[]{:S(2)}, u32[]{:S(2)}) collective-permute-start(bf16[512,1152]{1,0:T(8,128)(2,1)} %param.11), channel_id=1, source_target_pairs={{0,1},{1,0},{2,3},{3,2},{4,5},{5,4},{6,7},{7,6},{8,9},{9,8},{10,11... | collective-permute-start | bytes 3538952 | tf_op jit(solution)/shard_map/ppermute | solution.py:20
  23.5 3.9 %copy-start.3 = (bf16[512,1152]{1,0:T(8,128)(2,1)}, bf16[512,1152]{1,0:T(8,128)(2,1)S(1)}, u32[]{:S(2)}) copy-start(bf16[512,1152]{1,0:T(8,128)(2,1)S(1)} %collective-permute-done) | copy-start | bytes 3538948
  27.4 53.0 %collective-permute-start.1 = (bf16[2,512,1152]{2,1,0:T(8,128)(2,1)}, bf16[2,512,1152]{2,1,0:T(8,128)(2,1)}, u32[]{:S(2)}, u32[]{:S(2)}) collective-permute-start(bf16[2,512,1152]{2,1,0:T(8,128)(2,1)} %maximum_select_fusion.2), channel_id=1, source_target_pairs={{0,2},{1,3},{2,0},{3,1},{4,6},{5,7},{6,4},{7,5},{8,10},{9,11},{10,... | collective-permute-start | bytes 7077896 | tf_op jit(solution)/shard_map/ppermute | solution.py:20
  34.4 4.8 %copy-start.8 = (s32[16]{0:T(128)S(1)}, s32[16]{0:T(128)}, u32[]{:S(2)}) copy-start(s32[16]{0:T(128)} %param.15) | copy-start | bytes 196
  34.4 6.2 %copy-start.2 = (bf16[512,1152]{1,0:T(8,128)(2,1)S(1)}, bf16[512,1152]{1,0:T(8,128)(2,1)}, u32[]{:S(2)}) copy-start(bf16[512,1152]{1,0:T(8,128)(2,1)} %param.11) | copy-start | bytes 3538948
  80.4 3.1 copy-start.5
  103.6 5.9 %copy-start.6 = (bf16[1,512,576]{1,2,0:T(8,128)(2,1)S(1)}, bf16[1,512,576]{1,2,0:T(8,128)(2,1)}, u32[]{:S(2)}) copy-start(bf16[1,512,576]{1,2,0:T(8,128)(2,1)} %get-tuple-element.17) | copy-start | bytes 1769476
  126.8 14.1 %copy-start.4 = (bf16[512,1152]{1,0:T(8,128)(2,1)S(1)}, bf16[512,1152]{1,0:T(8,128)(2,1)}, u32[]{:S(2)}) copy-start(bf16[512,1152]{1,0:T(8,128)(2,1)} %param.10) | copy-start | bytes 3538948
  142.4 1.4 copy-start.1
  149.2 133.7 %copy-start.7 = (bf16[3,1152,576]{1,2,0:T(8,128)(2,1)S(1)}, bf16[3,1152,576]{1,2,0:T(8,128)(2,1)}, u32[]{:S(2)}) copy-start(bf16[3,1152,576]{1,2,0:T(8,128)(2,1)} %param.18) | copy-start | bytes 11943940
where the time goes:
time: 389 us; the launch traced here: 387 us
  blocking collectives  219 us (56%)
  matrix products  52.5 us (13%)
  waiting for transfers between devices  37.7 us (10%)
  local copies, waits for them, and re-layouts  37.1 us (10%)
  starting transfers between devices  20.4 us (5%)
  other arithmetic  18.3 us (5%)
    all_to_all x2, blocking collectives, moved_by_axis(): lax.all_to_all(parts, axes[k], split_axis=k, concat_axis=k, tiled=True)  139 us
    all_to_all x1, blocking collectives, per_device(): lax.all_to_all(mixed_out.reshape(devices, piece_rows, width_win), PATCH,...  80.3 us
    ppermute x2, waiting for transfers between devices, from_partner(): return lax.ppermute(value, axis, pairs)  37.7 us
    sub x2, matrix products, softmax_rows(): exp_scores = jnp.exp(scores - row_top)  22.1 us
    ppermute x2, starting transfers between devices, from_partner(): return lax.ppermute(value, axis, pairs)  20.4 us
    dot_general x1, matrix products, spatial_attend(): jnp.einsum('hqk,khe->qhe', weights, value_heads, preferred_element_type=j...  14.1 us
    select_n x3, other arithmetic, per_device(): jnp.where(low_half, jnp.stack([kv_block, partner], 0), jnp.stack([partner...  8.99 us
  transfers between devices with their start and end apart: 2, of which 1 were waited for; matrix products, arithmetic and copies ran while one was open for 4% of the time, Pallas kernels for 0%

commit v1 on v0

v1 whole, which is shorter than its diff:
```python
import functools
import math

import jax
import jax.numpy as jnp
from jax import lax
from jax.experimental import pallas as pl
from jax.experimental.pallas import tpu as pltpu
from jax.sharding import PartitionSpec as P

HEADS = 16
EPS = 1e-06
MESH = pl.DeviceIdType.MESH
F32 = jnp.float32
BF16 = jnp.bfloat16
LANES = 128
WINDOW = 256
TURNS = 2
KV_ROWS = (0, 256, 512)
NEG = -1e30


def sinusoid(position, feature_width):
    half_width = feature_width // 2
    frequencies = jnp.exp(
        -math.log(10000.0) * jnp.arange(half_width, dtype=F32) / half_width
    )
    angles = jnp.asarray(position).astype(F32)[..., None] * frequencies
    return jnp.concatenate([jnp.sin(angles), jnp.cos(angles)], axis=-1)


def normalize(v):
    inverse = 1.0 / v.shape[-1]
    mean = jnp.sum(v, axis=-1, keepdims=True) * inverse
    centered = v - mean
    variance = jnp.sum(centered * centered, axis=-1, keepdims=True) * inverse
    return centered * lax.rsqrt(variance + EPS)


def dot(a, b):
    return jnp.dot(a, b, preferred_element_type=F32)


def dot_t(a, b):
    return lax.dot_general(a, b, (((1,), (1,)), ((), ())), preferred_element_type=F32)


def window_start(column, most):
    return pl.multiple_of(jnp.minimum(column // LANES, most) * LANES, LANES)


def wide(x, width):
    return jnp.concatenate([x] * (width // LANES), axis=1) if width > LANES else x


def kernel(
    tokens, stale, mods, wqkv, wout, tqkv, tout, out,
    tok, kvb, wq, wo, tw, two, xin, qb, qm, mx, sm, acc, mixed, after, xs, xr,
    tq, tk, tv, tmix, osend, orecv, obuf,
    load_sem, kv_send, kv_recv, part_recv, fwd_recv, x_send, x_recv, o_send, o_recv, out_sem,
):
    rows, width = tok.shape
    win = wout.shape[0]
    head_dim = width // HEADS
    heads = win // head_dim
    devices = lax.axis_size("patch")
    frames = devices // 4
    piece = rows // frames // TURNS
    chunk = rows // (2 * TURNS)
    scale = head_dim ** (-0.5) * math.log2(math.e)
    me = lax.axis_index("patch")
    frame, quarter = me // 4, me % 4
    partner = frame * 4 + quarter + 1 - 2 * (quarter % 2)
    across = quarter + 2 - 4 * (quarter // 2)
    opposite = frame * 4 + across
    kv_most = width // LANES - WINDOW // LANES
    q_most = qb.shape[1] // LANES - WINDOW // LANES
    v_tile0 = win // LANES
    pad = win - v_tile0 * LANES

    def remote(src, dst, send, recv, device):
        return pltpu.make_async_remote_copy(
            src_ref=src, dst_ref=dst, send_sem=send, recv_sem=recv,
            device_id={"patch": device}, device_id_type=MESH,
        )

    loads = [
        (tokens, tok), (wqkv, wq), (wout, wo.at[pl.ds(pad, win), :]), (tqkv, tw), (tout, two),
    ]
    loads = [pltpu.make_async_copy(a, b, load_sem.at[i]) for i, (a, b) in enumerate(loads)]
    for copy in loads:
        copy.start()

    barrier = pltpu.get_barrier_semaphore()
    pl.semaphore_signal(barrier, inc=1, device_id={"patch": partner}, device_id_type=MESH)

    def greet(j, c):
        pl.semaphore_signal(
            barrier, inc=1, device_id={"patch": j * 4 + across}, device_id_type=MESH
        )
        return c

    lax.fori_loop(0, frames, greet, 0)
    pl.semaphore_wait(barrier, frames + 1)

    kv_pieces = list(zip(KV_ROWS[:-1], KV_ROWS[1:]))
    for n, (lo, hi) in enumerate(kv_pieces):
        part = stale.at[pl.ds(lo, hi - lo), :]
        remote(part, kvb.at[2, pl.ds(lo, hi - lo), :], kv_send.at[0], kv_recv.at[n], opposite).start()
    remote(stale, kvb.at[1], kv_send.at[1], part_recv, partner).start()

    wo[pl.ds(0, pad), :] = jnp.zeros((pad, width), BF16)
    for ref in (qb, tq, tk, tv):
        ref[...] = jnp.zeros(ref.shape, ref.dtype)
    mixed[...] = jnp.zeros(mixed.shape, mixed.dtype)

    shift_s, scale_s, gate_s = mods[0:1, :], mods[1:2, :], mods[2:3, :]
    shift_t, scale_t, gate_t = mods[3:4, :], mods[4:5, :], mods[5:6, :]

    loads[0].wait()

    def fresh_in(i, c):
        at = pl.ds(pl.multiple_of(i * chunk, chunk), chunk)
        v = normalize(tok[at, :].astype(F32))
        xin[at, :] = (v * scale_s + shift_s).astype(BF16)
        return c

    lax.fori_loop(0, rows // chunk, fresh_in, 0)
    loads[1].wait()

    def fresh(i, c):
        at = pl.ds(pl.multiple_of(i * WINDOW, WINDOW), WINDOW)
        x = xin[at, :]
        qb[at, 0:win] = dot_t(x, wq[0]).astype(BF16)
        kvb[0, at, 0:win] = dot_t(x, wq[1]).astype(BF16)
        kvb[0, at, win : 2 * win] = dot_t(x, wq[2]).astype(BF16)
        return c

    lax.fori_loop(0, rows // WINDOW, fresh, 0)

    def of_head(start, column, count):
        lane = lax.broadcasted_iota(jnp.int32, (count, WINDOW), 1) + start
        return (lane >= column) & (lane < column + head_dim)

    def mask_q(h, c):
        start = window_start(h * head_dim, q_most)
        q = qb[:, pl.ds(start, WINDOW)]
        qm[h] = jnp.where(of_head(start, h * head_dim, rows), q, jnp.zeros_like(q))
        mx[h] = jnp.full((rows, LANES), NEG, F32)
        sm[h] = jnp.zeros((rows, LANES), F32)
        acc[h] = jnp.zeros((rows, WINDOW), F32)
        return c

    lax.fori_loop(0, heads, mask_q, 0)

    def attend(h, blocks):
        k_at = window_start(h * head_dim, q_most)
        v_at = window_start(win + h * head_dim, kv_most)
        q = qm[h]
        scores = [dot_t(q, kvb[s, at, pl.ds(k_at, WINDOW)]) for s, at in blocks]
        top = jnp.max(scores[0], axis=-1, keepdims=True)
        for s in scores[1:]:
            top = jnp.maximum(top, jnp.max(s, axis=-1, keepdims=True))
        old = mx[h]
        new = jnp.maximum(old, top)
        mx[h] = new
        fade = jnp.exp2((old - new) * scale)
        total = 0.0
        product = 0.0
        for (s, at), score in zip(blocks, scores):
            e = jnp.exp2((score - wide(new, score.shape[1])) * scale)
            total = total + jnp.sum(e, axis=-1, keepdims=True)
            product = product + dot(e.astype(BF16), kvb[s, at, pl.ds(v_at, WINDOW)])
        sm[h] = sm[h] * fade + total
        acc[h] = acc[h] * wide(fade, WINDOW) + product

    whole = pl.ds(0, rows)
    lax.fori_loop(0, heads, lambda h, c: (attend(h, [(0, whole)]), c)[1], 0)
    remote(stale, kvb.at[1], kv_send.at[1], part_recv, partner).wait_recv()
    lax.fori_loop(0, heads, lambda h, c: (attend(h, [(1, whole)]), c)[1], 0)

    for n, (lo, hi) in enumerate(kv_pieces):
        at = pl.ds(lo, hi - lo)
        remote(stale.at[at, :], kvb.at[2, at, :], kv_send.at[0], kv_recv.at[n], opposite).wait_recv()
        forward = remote(
            kvb.at[2, at, :], kvb.at[3, at, :], kv_send.at[2], fwd_recv.at[n], partner
        )
        forward.start()
        forward.wait_recv()
        lax.fori_loop(0, heads, lambda h, c: (attend(h, [(2, at), (3, at)]), c)[1], 0)

    loads[2].wait()

    def finish(u, c):
        at = pl.ds(pl.multiple_of(u * chunk, chunk), chunk)

        def place(h, c):
            v_at = window_start(win + h * head_dim, kv_most)
            m_at = pl.ds(pl.multiple_of(v_at - v_tile0 * LANES, LANES), WINDOW)
            value = (acc[h, at, :] / wide(sm[h, at, :], WINDOW)).astype(BF16)
            keep = of_head(v_at, win + h * head_dim, chunk)
            mixed[at, m_at] = jnp.where(keep, value, mixed[at, m_at])
            return c

        lax.fori_loop(0, heads, place, 0)
        done = tok[at, :].astype(F32) + gate_s * dot(mixed[at, :], wo[...])
        after[at, :] = done
        xs[at, :] = (normalize(done) * scale_t + shift_t).astype(BF16)
        turn = u // 2
        for i in (3, 4, 2, 5, 1, 6, 0, 7):
            m = 2 * i + (u + frame) % 2
            j = (frame + m) % frames
            src = pl.ds(pl.multiple_of(u * chunk + (j // 2) * piece, piece), piece)
            remote(
                xs.at[src, :], xr.at[turn, frame], x_send, x_recv.at[turn], j * 4 + across
            ).start()
        return c

    lax.fori_loop(0, 2 * TURNS, finish, 0)

    loads[3].wait()
    block = frames * piece
    same = (
        lax.broadcasted_iota(jnp.int32, (block, block), 0) % piece
        == lax.broadcasted_iota(jnp.int32, (block, block), 1) % piece
    )

    def temporal(turn, c):
        remote(xr.at[turn], xr.at[turn], x_send, x_recv.at[turn], opposite).wait_recv()
        x = xr[turn].reshape(block, width)
        tq[:, 0:win] = dot_t(x, tw[0]).astype(BF16)
        tk[:, 0:win] = dot_t(x, tw[1]).astype(BF16)
        tv[:, 0:win] = dot_t(x, tw[2]).astype(BF16)

        def one_head(h, c):
            start = window_start(h * head_dim, q_most)
            at = pl.ds(start, WINDOW)
            keep = of_head(start, h * head_dim, block)
            q = tq[:, at]
            score = dot_t(jnp.where(keep, q, jnp.zeros_like(q)), tk[:, at])
            score = jnp.where(same, score, NEG)
            top = jnp.max(score, axis=-1, keepdims=True)
            e = jnp.where(same, jnp.exp2((score - top) * scale), 0.0)
            weights = (e / jnp.sum(e, axis=-1, keepdims=True)).astype(BF16)
            value = dot(weights, tv[:, at]).astype(BF16)
            tmix[:, at] = jnp.where(keep, value, tmix[:, at])
            return c

        lax.fori_loop(0, heads, one_head, 0)
        osend[turn] = tmix[:, 0:win].reshape(frames, piece, win)
        row = turn * (rows // TURNS) + (frame % 2) * chunk + (frame // 2) * piece
        row = pl.multiple_of(row, piece)
        for i in (7, 8, 6, 9, 5, 10, 4, 11, 3, 12, 2, 13, 1, 14, 0, 15):
            j = (frame + i) % frames
            remote(
                osend.at[turn, j], orecv.at[pl.ds(row, piece), :], o_send, o_recv.at[turn],
                j * 4 + across,
            ).start()
        return c

    tmix[...] = jnp.zeros(tmix.shape, tmix.dtype)
    lax.fori_loop(0, TURNS, temporal, 0)

    loads[4].wait()
    half = rows // TURNS

    def last(turn, c):
        at = pl.ds(pl.multiple_of(turn * half, half), half)
        remote(orecv.at[at, :], orecv.at[at, :], o_send, o_recv.at[turn], opposite).wait_recv()
        obuf[at, :] = after[at, :] + gate_t * dot(orecv[at, :], two[...])
        pltpu.make_async_copy(obuf.at[at, :], out.at[at, :], out_sem).start()
        return c

    lax.fori_loop(0, TURNS, last, 0)
    pltpu.make_async_copy(obuf, out, out_sem).wait()
    remote(stale, kvb.at[2], kv_send.at[0], kv_recv.at[0], opposite).wait_send()
    remote(stale, kvb.at[1], kv_send.at[1], part_recv, partner).wait_send()
    remote(kvb.at[2], kvb.at[3], kv_send.at[2], fwd_recv.at[0], partner).wait_send()
    remote(xs, xs, x_send, x_recv.at[0], opposite).wait_send()
    remote(osend, osend, o_send, o_recv.at[0], opposite).wait_send()


def per_device(
    tokens, stale_kv, mod_table, mod_mix, timestep, frame_order,
    spatial_qkv, spatial_out, temporal_qkv, temporal_out,
):
    rows, width = tokens.shape
    win = spatial_out.shape[0]
    heads = win // (width // HEADS)
    frames = lax.axis_size("patch") // 4
    piece = rows // frames // TURNS
    frame = lax.axis_index("patch") // 4
    modulation = mod_table + mod_mix * sinusoid(timestep[0], width)[None, :]
    frame_id = jnp.sum(jnp.where(jnp.arange(frames) == frame, frame_order, 0))
    emb = sinusoid(frame_id, width)
    row_id = jnp.arange(8)[:, None]
    mods = jnp.concatenate([modulation, modulation[:2]], axis=0)
    mods = mods + jnp.where((row_id == 1) | (row_id == 4), 1.0, 0.0)
    mods = mods + jnp.where(row_id == 3, emb[None, :], 0.0)
    padded = -(-win // LANES) * LANES
    block = frames * piece
    any_spec = pl.BlockSpec(memory_space=pl.ANY)
    pieces = len(KV_ROWS) - 1
    dma = pltpu.SemaphoreType.DMA
    return pl.pallas_call(
        kernel,
        out_shape=jax.ShapeDtypeStruct((rows, width), F32),
        in_specs=[any_spec, any_spec, pl.BlockSpec(memory_space=pltpu.VMEM)] + [any_spec] * 4,
        out_specs=any_spec,
        scratch_shapes=[
            pltpu.VMEM((rows, width), BF16),
            pltpu.VMEM((4, rows, width), BF16),
            pltpu.VMEM((3, win, width), BF16),
            pltpu.VMEM((padded, width), BF16),
            pltpu.VMEM((3, win, width), BF16),
            pltpu.VMEM((win, width), BF16),
            pltpu.VMEM((rows, width), BF16),
            pltpu.VMEM((rows, padded), BF16),
            pltpu.VMEM((heads, rows, WINDOW), BF16),
            pltpu.VMEM((heads, rows, LANES), F32),
            pltpu.VMEM((heads, rows, LANES), F32),
            pltpu.VMEM((heads, rows, WINDOW), F32),
            pltpu.VMEM((rows, padded), BF16),
            pltpu.VMEM((rows, width), F32),
            pltpu.VMEM((rows, width), BF16),
            pltpu.VMEM((TURNS, frames, piece, width), BF16),
            pltpu.VMEM((block, padded), BF16),
            pltpu.VMEM((block, padded), BF16),
            pltpu.VMEM((block, padded), BF16),
            pltpu.VMEM((block, padded), BF16),
            pltpu.VMEM((TURNS, frames, piece, win), BF16),
            pltpu.VMEM((rows, win), BF16),
            pltpu.VMEM((rows, width), F32),
            dma((5,)), dma((3,)), dma((pieces,)), dma, dma((pieces,)),
            dma, dma((TURNS,)), dma, dma((TURNS,)), dma,
        ],
        compiler_params=pltpu.CompilerParams(
            collective_id=0, has_side_effects=True, vmem_limit_bytes=60 * 1024 * 1024
        ),
        name="block",
    )(
        tokens, stale_kv, mods, jnp.swapaxes(spatial_qkv, 1, 2), spatial_out,
        jnp.swapaxes(temporal_qkv, 1, 2), temporal_out,
    )


def solution(mesh):
    return jax.shard_map(
        per_device,
        mesh=mesh,
        in_specs=(
            P(("groups", "patch"), None), P(("groups", "patch"), None), P(), P(),
            P("groups"), P("groups"), P(), P(), P(), P(),
        ),
        out_specs=P(("groups", "patch"), None),
        check_vma=False,
    )
```

time: 389 us -> 238 us (0.61)
  Pallas kernels: 0 us -> 229 us
  blocking collectives: 219 us -> 0 us
  matrix products: 52.5 us -> 0 us
  waiting for transfers between devices: 37.7 us -> 0 us
  local copies, waits for them, and re-layouts: 37.1 us -> 3.23 us
  starting transfers between devices: 20.4 us -> 0 us
  other arithmetic: 18.3 us -> 3.14 us
    pallas_call x0 -> x1, Pallas kernels: none -> 229 us  [per_device(): pl.pallas_call(kernel, out_shape=jax.ShapeDtypeStruct((rows, width), F32)...]
    all_to_all x3 -> x0, blocking collectives: 219 us -> none  [the longest x2 139 us: moved_by_axis(): lax.all_to_all(parts, axes[k], split_axis=k, concat_axis=k, tiled=True)]
    ppermute x2 -> x0, waiting for transfers between devices: 37.7 us -> none  [from_partner(): return lax.ppermute(value, axis, pairs)]
    dot_general x6 -> x0, matrix products: 30.4 us -> none  [the longest x1 14.1 us: spatial_attend(): jnp.einsum('hqk,khe->qhe', weights, value_heads, preferred_element_type=j...]
    sub x2 -> x0, matrix products: 22.1 us -> none  [softmax_rows(): exp_scores = jnp.exp(scores - row_top)]
    ppermute x2 -> x0, starting transfers between devices: 20.4 us -> none  [from_partner(): return lax.ppermute(value, axis, pairs)]
    another operation x6 -> x0, local copies, waits for them, and re-layouts: 16.9 us -> none  [the longest x1 5.92 us: spatial_attend(): key_heads = key_rows.reshape(-1, head_count, head_dim)]
    select_n x4 -> x1, other arithmetic: 12.4 us -> 0.01 us  [per_device(): mods = mods + jnp.where((row_id == 1) | (row_id == 4), 1.0, 0.0)]
  transfers between devices with their start and end apart: 2 -> 0, of which waited for: 1 -> 0; matrix products, arithmetic and copies ran while one was open for 4% -> 0% of each run, Pallas kernels for 0% -> 0%
where the time goes in v1:
time: 238 us; the launch traced here: 237 us
  Pallas kernels  229 us (96%)
  local copies, waits for them, and re-layouts  3.23 us (1%)
  other arithmetic  3.14 us (1%)
    pallas_call x1, Pallas kernels, per_device(): pl.pallas_call(kernel, out_shape=jax.ShapeDtypeStruct((rows, width), F32)...  229 us

profile of v1, /device:TPU:37, one launch (start us, length us, event | category | flops | bytes accessed | tf_op | source)
XLA Modules:
  0.0 236.9 jit_solution(8758544598759997251)
XLA Ops:
  0.7 1.4 fusion.7
  2.7 0.1 fusion.5
  2.8 0.1 pad_maximum_fusion.1
  2.9 0.1 fusion.3
  2.9 0.1 pad_maximum_fusion
  3.0 0.8 multiply_add_fusion
  3.8 0.7 fusion.mods
  4.5 229.2 %block.1 = f32[512,1152]{1,0:T(8,128)} custom-call(bf16[512,1152]{1,0:T(8,128)(2,1)} %tokens.1, bf16[512,1152]{1,0:T(8,128)(2,1)} %stale.1, f32[8,1152]{1,0:T(8,128)} %fusion.mods, bf16[3,576,1152]{2,1,0:T(8,128)(2,1)} %bitcast.3, bf16[576,1152]{1,0:T(8,128)(2,1)} %wout.1, bf16[3,576,1152]{2,1,0:T(8,128)(2,1)} %bitcast.4, bf16[576,1152]{1,0:T(8,128)(2,1)} %tout.1), custom_call_target="tpu_custom_call" | custom-call | tf_op jit(solution)/shard_map/block/pallas_call | solution.py:305
  233.7 3.2 %copy.13 = f32[512,1152]{1,0:T(8,128)} copy(f32[512,1152]{1,0:T(8,128)} %block.1) | data formatting | bytes 4718592
  (3 shorter events, 0.0 us)

commit v2 on v1

--- a/solution.py
+++ b/solution.py
@@ -15,8 +15,9 @@
 BF16 = jnp.bfloat16
 LANES = 128
 WINDOW = 256
+UNROLL = 8
 TURNS = 2
-KV_ROWS = (0, 256, 512)
+KV_ROWS = (0, 256, 384, 512)
 NEG = -1e30
 
 
@@ -56,8 +57,8 @@
 def kernel(
     tokens, stale, mods, wqkv, wout, tqkv, tout, out,
     tok, kvb, wq, wo, tw, two, xin, qb, qm, mx, sm, acc, mixed, after, xs, xr,
-    tq, tk, tv, tmix, osend, orecv, obuf,
-    load_sem, kv_send, kv_recv, part_recv, fwd_recv, x_send, x_recv, o_send, o_recv, out_sem,
+    tq, tk, tv, tmix, osend, orecv,
+    load_sem, kv_send, kv_recv, part_recv, fwd_recv, x_send, x_recv, o_send, o_recv, known,
 ):
     rows, width = tok.shape
     win = wout.shape[0]
@@ -85,23 +86,32 @@
         )
 
     loads = [
-        (tokens, tok), (wqkv, wq), (wout, wo.at[pl.ds(pad, win), :]), (tqkv, tw), (tout, two),
+        (tokens, tok), (wqkv, wq), (wout, wo.at[pl.ds(pad, win), :]), (tqkv, tw), (tout, two.at[pl.ds(0, win), :]),
     ]
     loads = [pltpu.make_async_copy(a, b, load_sem.at[i]) for i, (a, b) in enumerate(loads)]
     for copy in loads:
         copy.start()
 
     barrier = pltpu.get_barrier_semaphore()
-    pl.semaphore_signal(barrier, inc=1, device_id={"patch": partner}, device_id_type=MESH)
-
-    def greet(j, c):
-        pl.semaphore_signal(
-            barrier, inc=1, device_id={"patch": j * 4 + across}, device_id_type=MESH
-        )
-        return c
-
-    lax.fori_loop(0, frames, greet, 0)
-    pl.semaphore_wait(barrier, frames + 1)
+    before, after_me = (frame + frames - 1) % frames, (frame + 1) % frames
+    near = [partner, opposite]
+    for j in (before, after_me):
+        near += [j * 4 + quarter, j * 4 + across]
+    for device in near:
+        pl.semaphore_signal(barrier, inc=1, device_id={"patch": device}, device_id_type=MESH)
+    pl.semaphore_wait(barrier, len(near))
+
+    distances = [1 << n for n in range(frames.bit_length() - 2)]
+
+    def say(n):
+        for away in (distances[n], frames - distances[n]):
+            j = (frame + away) % frames
+            pl.semaphore_signal(
+                known.at[n], inc=1, device_id={"patch": j * 4 + quarter}, device_id_type=MESH
+            )
+
+    def hear(n):
+        pl.semaphore_wait(known.at[n], 2)
 
     kv_pieces = list(zip(KV_ROWS[:-1], KV_ROWS[1:]))
     for n, (lo, hi) in enumerate(kv_pieces):
@@ -109,7 +119,10 @@
         remote(part, kvb.at[2, pl.ds(lo, hi - lo), :], kv_send.at[0], kv_recv.at[n], opposite).start()
     remote(stale, kvb.at[1], kv_send.at[1], part_recv, partner).start()
 
+    say(0)
+
     wo[pl.ds(0, pad), :] = jnp.zeros((pad, width), BF16)
+    two[pl.ds(win, two.shape[0] - win), :] = jnp.zeros((two.shape[0] - win, width), BF16)
     for ref in (qb, tq, tk, tv):
         ref[...] = jnp.zeros(ref.shape, ref.dtype)
     mixed[...] = jnp.zeros(mixed.shape, mixed.dtype)
@@ -126,6 +139,8 @@
         return c
 
     lax.fori_loop(0, rows // chunk, fresh_in, 0)
+    hear(0)
+    say(1)
     loads[1].wait()
 
     def fresh(i, c):
@@ -137,10 +152,18 @@
         return c
 
     lax.fori_loop(0, rows // WINDOW, fresh, 0)
+    for n in range(1, len(distances) - 1):
+        hear(n)
+        say(n + 1)
+
+    whole = pl.ds(0, rows)
 
     def of_head(start, column, count):
         lane = lax.broadcasted_iota(jnp.int32, (count, WINDOW), 1) + start
         return (lane >= column) & (lane < column + head_dim)
+
+    def each_head(step):
+        lax.fori_loop(0, heads, lambda h, c: (step(h), c)[1], 0, unroll=UNROLL)
 
     def mask_q(h, c):
         start = window_start(h * head_dim, q_most)
@@ -153,17 +176,17 @@
 
     lax.fori_loop(0, heads, mask_q, 0)
 
-    def attend(h, blocks):
+    def attend(h, blocks, own=whole):
         k_at = window_start(h * head_dim, q_most)
         v_at = window_start(win + h * head_dim, kv_most)
-        q = qm[h]
+        q = qm[h, own, :]
         scores = [dot_t(q, kvb[s, at, pl.ds(k_at, WINDOW)]) for s, at in blocks]
         top = jnp.max(scores[0], axis=-1, keepdims=True)
         for s in scores[1:]:
             top = jnp.maximum(top, jnp.max(s, axis=-1, keepdims=True))
-        old = mx[h]
+        old = mx[h, own, :]
         new = jnp.maximum(old, top)
-        mx[h] = new
+        mx[h, own, :] = new
         fade = jnp.exp2((old - new) * scale)
         total = 0.0
         product = 0.0
@@ -171,13 +194,12 @@
             e = jnp.exp2((score - wide(new, score.shape[1])) * scale)
             total = total + jnp.sum(e, axis=-1, keepdims=True)
             product = product + dot(e.astype(BF16), kvb[s, at, pl.ds(v_at, WINDOW)])
-        sm[h] = sm[h] * fade + total
-        acc[h] = acc[h] * wide(fade, WINDOW) + product
-
-    whole = pl.ds(0, rows)
-    lax.fori_loop(0, heads, lambda h, c: (attend(h, [(0, whole)]), c)[1], 0)
+        sm[h, own, :] = sm[h, own, :] * fade + total
+        acc[h, own, :] = acc[h, own, :] * wide(fade, WINDOW) + product
+
+    each_head(lambda h: attend(h, [(0, whole)]))
     remote(stale, kvb.at[1], kv_send.at[1], part_recv, partner).wait_recv()
-    lax.fori_loop(0, heads, lambda h, c: (attend(h, [(1, whole)]), c)[1], 0)
+    each_head(lambda h: attend(h, [(1, whole)]))
 
     for n, (lo, hi) in enumerate(kv_pieces):
         at = pl.ds(lo, hi - lo)
@@ -187,22 +209,27 @@
         )
         forward.start()
         forward.wait_recv()
-        lax.fori_loop(0, heads, lambda h, c: (attend(h, [(2, at), (3, at)]), c)[1], 0)
+        if hi < rows:
+            each_head(lambda h: attend(h, [(2, at), (3, at)]))
 
     loads[2].wait()
+
+    for n in range(max(len(distances) - 1, 0), len(distances)):
+        hear(n)
+    final = pl.ds(kv_pieces[-1][0], rows - kv_pieces[-1][0])
 
     def finish(u, c):
         at = pl.ds(pl.multiple_of(u * chunk, chunk), chunk)
-
-        def place(h, c):
+        each_head(lambda h: attend(h, [(2, final), (3, final)], at))
+
+        def place(h):
             v_at = window_start(win + h * head_dim, kv_most)
             m_at = pl.ds(pl.multiple_of(v_at - v_tile0 * LANES, LANES), WINDOW)
             value = (acc[h, at, :] / wide(sm[h, at, :], WINDOW)).astype(BF16)
             keep = of_head(v_at, win + h * head_dim, chunk)
             mixed[at, m_at] = jnp.where(keep, value, mixed[at, m_at])
-            return c
-
-        lax.fori_loop(0, heads, place, 0)
+
+        each_head(place)
         done = tok[at, :].astype(F32) + gate_s * dot(mixed[at, :], wo[...])
         after[at, :] = done
         xs[at, :] = (normalize(done) * scale_t + shift_t).astype(BF16)
@@ -219,6 +246,7 @@
     lax.fori_loop(0, 2 * TURNS, finish, 0)
 
     loads[3].wait()
+    full = win // LANES
     block = frames * piece
     same = (
         lax.broadcasted_iota(jnp.int32, (block, block), 0) % piece
@@ -232,7 +260,7 @@
         tk[:, 0:win] = dot_t(x, tw[1]).astype(BF16)
         tv[:, 0:win] = dot_t(x, tw[2]).astype(BF16)
 
-        def one_head(h, c):
+        def one_head(h):
             start = window_start(h * head_dim, q_most)
             at = pl.ds(start, WINDOW)
             keep = of_head(start, h * head_dim, block)
@@ -244,16 +272,22 @@
             weights = (e / jnp.sum(e, axis=-1, keepdims=True)).astype(BF16)
             value = dot(weights, tv[:, at]).astype(BF16)
             tmix[:, at] = jnp.where(keep, value, tmix[:, at])
-            return c
-
-        lax.fori_loop(0, heads, one_head, 0)
-        osend[turn] = tmix[:, 0:win].reshape(frames, piece, win)
-        row = turn * (rows // TURNS) + (frame % 2) * chunk + (frame // 2) * piece
-        row = pl.multiple_of(row, piece)
+
+        each_head(one_head)
+        for n in range(full):
+            part = tmix[:, n * LANES : (n + 1) * LANES]
+            osend[turn, :, n * piece : (n + 1) * piece, :] = part.reshape(frames, piece, LANES)
+        tail = tmix[:, full * LANES : (full + 1) * LANES].astype(F32)
+        tail = tail.reshape(frames, 2, piece // 2, LANES)
+        tail = tail[:, 0] + pltpu.roll(tail[:, 1].reshape(block // 2, LANES), LANES // 2, 1).reshape(
+            frames, piece // 2, LANES
+        )
+        osend[turn, :, full * piece :, :] = tail.astype(BF16)
+        slot = (frame % 2) * (frames // 2) + frame // 2
         for i in (7, 8, 6, 9, 5, 10, 4, 11, 3, 12, 2, 13, 1, 14, 0, 15):
             j = (frame + i) % frames
             remote(
-                osend.at[turn, j], orecv.at[pl.ds(row, piece), :], o_send, o_recv.at[turn],
+                osend.at[turn, j], orecv.at[turn, slot], o_send, o_recv.at[turn],
                 j * 4 + across,
             ).start()
         return c
@@ -266,13 +300,19 @@
 
     def last(turn, c):
         at = pl.ds(pl.multiple_of(turn * half, half), half)
-        remote(orecv.at[at, :], orecv.at[at, :], o_send, o_recv.at[turn], opposite).wait_recv()
-        obuf[at, :] = after[at, :] + gate_t * dot(orecv[at, :], two[...])
-        pltpu.make_async_copy(obuf.at[at, :], out.at[at, :], out_sem).start()
+        remote(orecv.at[turn], orecv.at[turn], o_send, o_recv.at[turn], opposite).wait_recv()
+        parts = [
+            orecv[turn, :, n * piece : (n + 1) * piece, :].reshape(half, LANES)
+            for n in range(full)
+        ]
+        tail = orecv[turn, :, full * piece :, :].astype(F32)
+        low = pltpu.roll(tail.reshape(half // 2, LANES), LANES // 2, 1)
+        tail = jnp.concatenate([tail, low.reshape(tail.shape)], axis=1)
+        parts.append(tail.reshape(half, LANES).astype(BF16))
+        out[at, :] = after[at, :] + gate_t * dot(jnp.concatenate(parts, axis=1), two[...])
         return c
 
     lax.fori_loop(0, TURNS, last, 0)
-    pltpu.make_async_copy(obuf, out, out_sem).wait()
     remote(stale, kvb.at[2], kv_send.at[0], kv_recv.at[0], opposite).wait_send()
     remote(stale, kvb.at[1], kv_send.at[1], part_recv, partner).wait_send()
     remote(kvb.at[2], kvb.at[3], kv_send.at[2], fwd_recv.at[0], partner).wait_send()
@@ -304,16 +344,16 @@
     dma = pltpu.SemaphoreType.DMA
     return pl.pallas_call(
         kernel,
-        out_shape=jax.ShapeDtypeStruct((rows, width), F32),
+        out_shape=pltpu.VMEM((rows, width), F32),
         in_specs=[any_spec, any_spec, pl.BlockSpec(memory_space=pltpu.VMEM)] + [any_spec] * 4,
-        out_specs=any_spec,
+        out_specs=pl.BlockSpec(memory_space=pltpu.VMEM),
         scratch_shapes=[
             pltpu.VMEM((rows, width), BF16),
             pltpu.VMEM((4, rows, width), BF16),
             pltpu.VMEM((3, win, width), BF16),
             pltpu.VMEM((padded, width), BF16),
             pltpu.VMEM((3, win, width), BF16),
-            pltpu.VMEM((win, width), BF16),
+            pltpu.VMEM((padded, width), BF16),
             pltpu.VMEM((rows, width), BF16),
             pltpu.VMEM((rows, padded), BF16),
             pltpu.VMEM((heads, rows, WINDOW), BF16),
@@ -328,14 +368,14 @@
             pltpu.VMEM((block, padded), BF16),
             pltpu.VMEM((block, padded), BF16),
             pltpu.VMEM((block, padded), BF16),
-            pltpu.VMEM((TURNS, frames, piece, win), BF16),
-            pltpu.VMEM((rows, win), BF16),
-            pltpu.VMEM((rows, width), F32),
+            pltpu.VMEM((TURNS, frames, piece * win // LANES, LANES), BF16),
+            pltpu.VMEM((TURNS, frames, piece * win // LANES, LANES), BF16),
             dma((5,)), dma((3,)), dma((pieces,)), dma, dma((pieces,)),
-            dma, dma((TURNS,)), dma, dma((TURNS,)), dma,
+            dma, dma((TURNS,)), dma, dma((TURNS,)),
+            pltpu.SemaphoreType.REGULAR((max(frames.bit_length() - 2, 1),)),
         ],
         compiler_params=pltpu.CompilerParams(
-            collective_id=0, has_side_effects=True, vmem_limit_bytes=60 * 1024 * 1024
+            collective_id=0, has_side_effects=True, vmem_limit_bytes=52 * 1024 * 1024
         ),
         name="block",
     )(

time: 238 us -> 217 us (0.912)
  Pallas kernels: 229 us -> 211 us
    pallas_call x1, Pallas kernels: 229 us -> 211 us  [per_device(): pl.pallas_call(kernel, out_shape=pltpu.VMEM((rows, width), F32), in_specs...]
where the time goes in v2:
time: 217 us
  Pallas kernels  211 us (97%)
  other arithmetic  3.14 us (1%)
    pallas_call x1, Pallas kernels, per_device(): pl.pallas_call(kernel, out_shape=pltpu.VMEM((rows, width), F32), in_specs...  211 us

profile of v2, /device:TPU:37, one launch (start us, length us, event | category | flops | bytes accessed | tf_op | source)
XLA Modules:
  0.0 217.1 jit_solution(5132029327251406269)
XLA Ops:
  0.7 1.4 fusion.7
  2.7 0.1 fusion.5
  2.8 0.1 pad_maximum_fusion.1
  2.9 0.1 fusion.3
  2.9 0.1 pad_maximum_fusion
  3.0 0.8 multiply_add_fusion
  3.8 0.7 fusion.mods
  4.5 211.1 %block.1 = f32[512,1152]{1,0:T(8,128)S(1)} custom-call(bf16[512,1152]{1,0:T(8,128)(2,1)} %tokens.1, bf16[512,1152]{1,0:T(8,128)(2,1)} %stale.1, f32[8,1152]{1,0:T(8,128)} %fusion.mods, bf16[3,576,1152]{2,1,0:T(8,128)(2,1)} %bitcast.3, bf16[576,1152]{1,0:T(8,128)(2,1)} %wout.1, bf16[3,576,1152]{2,1,0:T(8,128)(2,1)} %bitcast.4, bf16[576,1152]{1,0:T(8,128)(2,1)} %tout.1), custom_call_target="tpu_custom_call" | custom-call | tf_op jit(solution)/shard_map/block/pallas_call | solution.py:345
  215.7 1.4 copy.12
  (3 shorter events, 0.0 us)

commit v3 on v2

--- a/solution.py
+++ b/solution.py
@@ -3,6 +3,7 @@
 
 import jax
 import jax.numpy as jnp
+import numpy as np
 from jax import lax
 from jax.experimental import pallas as pl
 from jax.experimental.pallas import tpu as pltpu
@@ -21,13 +22,29 @@
 NEG = -1e30
 
 
-def sinusoid(position, feature_width):
+def angular_rates(feature_width):
     half_width = feature_width // 2
-    frequencies = jnp.exp(
-        -math.log(10000.0) * jnp.arange(half_width, dtype=F32) / half_width
-    )
-    angles = jnp.asarray(position).astype(F32)[..., None] * frequencies
-    return jnp.concatenate([jnp.sin(angles), jnp.cos(angles)], axis=-1)
+    rates = np.exp(-math.log(10000.0) * np.arange(half_width, dtype=np.float64) / half_width)
+    return np.concatenate([rates, rates]).astype(np.float32)[None, :]
+
+
+def sinusoid(position, rates):
+    width = rates.shape[1]
+    upper = lax.broadcasted_iota(jnp.int32, (1, width), 1) >= width // 2
+    angle = position.astype(F32) * rates
+    turn = jnp.floor(angle * (2.0 / math.pi) + 0.5)
+    x = angle - turn * 1.5703125
+    x = x - turn * 4.837512969970703125e-4
+    x = x - turn * 7.54978995489188216e-8
+    z = x * x
+    sine = ((-1.9515295891e-4 * z + 8.3321608736e-3) * z - 1.6666654611e-1) * z * x + x
+    cosine = (2.443315711809948e-5 * z - 1.388731625493765e-3) * z + 4.166664568298827e-2
+    cosine = cosine * z * z - 0.5 * z + 1.0
+    quarter = turn + jnp.where(upper, 1.0, 0.0)
+    quarter = quarter - 4.0 * jnp.floor(quarter * 0.25)
+    odd = (quarter == 1.0) | (quarter == 3.0)
+    value = jnp.where(odd, cosine, sine)
+    return jnp.where(quarter >= 2.0, -value, value)
 
 
 def normalize(v):
@@ -55,10 +72,11 @@
 
 
 def kernel(
-    tokens, stale, mods, wqkv, wout, tqkv, tout, out,
+    tokens, stale, table_in, mix_in, time_in, order_in, rates_in, wqkv, wout, tqkv, tout, out,
+    table, mix, time, order, rates, mods,
     tok, kvb, wq, wo, tw, two, xin, qb, qm, mx, sm, acc, mixed, after, xs, xr,
     tq, tk, tv, tmix, osend, orecv,
-    load_sem, kv_send, kv_recv, part_recv, fwd_recv, x_send, x_recv, o_send, o_recv, known,
+    small_sem, load_sem, kv_send, kv_recv, part_recv, fwd_recv, x_send, x_recv, o_send, o_recv, known,
 ):
     rows, width = tok.shape
     win = wout.shape[0]
@@ -85,13 +103,6 @@
             device_id={"patch": device}, device_id_type=MESH,
         )
 
-    loads = [
-        (tokens, tok), (wqkv, wq), (wout, wo.at[pl.ds(pad, win), :]), (tqkv, tw), (tout, two.at[pl.ds(0, win), :]),
-    ]
-    loads = [pltpu.make_async_copy(a, b, load_sem.at[i]) for i, (a, b) in enumerate(loads)]
-    for copy in loads:
-        copy.start()
-
     barrier = pltpu.get_barrier_semaphore()
     before, after_me = (frame + frames - 1) % frames, (frame + 1) % frames
     near = [partner, opposite]
@@ -99,6 +110,17 @@
         near += [j * 4 + quarter, j * 4 + across]
     for device in near:
         pl.semaphore_signal(barrier, inc=1, device_id={"patch": device}, device_id_type=MESH)
+
+    loads = [
+        (tokens, tok), (wqkv, wq), (wout, wo.at[pl.ds(pad, win), :]), (tqkv, tw), (tout, two.at[pl.ds(0, win), :]),
+    ]
+    small = [
+        (table_in, table), (mix_in, mix), (time_in, time), (order_in, order), (rates_in, rates),
+    ]
+    small = [pltpu.make_async_copy(a, b, small_sem.at[i]) for i, (a, b) in enumerate(small)]
+    loads = [pltpu.make_async_copy(a, b, load_sem.at[i]) for i, (a, b) in enumerate(loads)]
+    for copy in loads[:1] + small + loads[1:]:
+        copy.start()
     pl.semaphore_wait(barrier, len(near))
 
     distances = [1 << n for n in range(frames.bit_length() - 2)]
@@ -127,8 +149,12 @@
         ref[...] = jnp.zeros(ref.shape, ref.dtype)
     mixed[...] = jnp.zeros(mixed.shape, mixed.dtype)
 
-    shift_s, scale_s, gate_s = mods[0:1, :], mods[1:2, :], mods[2:3, :]
-    shift_t, scale_t, gate_t = mods[3:4, :], mods[4:5, :], mods[5:6, :]
+    for copy in small:
+        copy.wait()
+    mods[...] = table[...] + mix[...] * sinusoid(time[0], rates[...])
+    position = sinusoid(order[frame], rates[...])
+    shift_s, scale_s, gate_s = mods[0:1, :], 1.0 + mods[1:2, :], mods[2:3, :]
+    shift_t, scale_t, gate_t = mods[3:4, :] + position, 1.0 + mods[4:5, :], mods[5:6, :]
 
     loads[0].wait()
 
@@ -329,14 +355,6 @@
     heads = win // (width // HEADS)
     frames = lax.axis_size("patch") // 4
     piece = rows // frames // TURNS
-    frame = lax.axis_index("patch") // 4
-    modulation = mod_table + mod_mix * sinusoid(timestep[0], width)[None, :]
-    frame_id = jnp.sum(jnp.where(jnp.arange(frames) == frame, frame_order, 0))
-    emb = sinusoid(frame_id, width)
-    row_id = jnp.arange(8)[:, None]
-    mods = jnp.concatenate([modulation, modulation[:2]], axis=0)
-    mods = mods + jnp.where((row_id == 1) | (row_id == 4), 1.0, 0.0)
-    mods = mods + jnp.where(row_id == 3, emb[None, :], 0.0)
     padded = -(-win // LANES) * LANES
     block = frames * piece
     any_spec = pl.BlockSpec(memory_space=pl.ANY)
@@ -345,9 +363,15 @@
     return pl.pallas_call(
         kernel,
         out_shape=pltpu.VMEM((rows, width), F32),
-        in_specs=[any_spec, any_spec, pl.BlockSpec(memory_space=pltpu.VMEM)] + [any_spec] * 4,
+        in_specs=[any_spec] * 2 + [pl.BlockSpec(memory_space=pltpu.HBM)] * 5 + [any_spec] * 4,
         out_specs=pl.BlockSpec(memory_space=pltpu.VMEM),
         scratch_shapes=[
+            pltpu.VMEM(mod_table.shape, F32),
+            pltpu.VMEM(mod_table.shape, F32),
+            pltpu.SMEM(timestep.shape, jnp.int32),
+            pltpu.SMEM(frame_order.shape, jnp.int32),
+            pltpu.VMEM((1, width), F32),
+            pltpu.VMEM(mod_table.shape, F32),
             pltpu.VMEM((rows, width), BF16),
             pltpu.VMEM((4, rows, width), BF16),
             pltpu.VMEM((3, win, width), BF16),
@@ -370,7 +394,7 @@
             pltpu.VMEM((block, padded), BF16),
             pltpu.VMEM((TURNS, frames, piece * win // LANES, LANES), BF16),
             pltpu.VMEM((TURNS, frames, piece * win // LANES, LANES), BF16),
-            dma((5,)), dma((3,)), dma((pieces,)), dma, dma((pieces,)),
+            dma((5,)), dma((5,)), dma((3,)), dma((pieces,)), dma, dma((pieces,)),
             dma, dma((TURNS,)), dma, dma((TURNS,)),
             pltpu.SemaphoreType.REGULAR((max(frames.bit_length() - 2, 1),)),
         ],
@@ -379,7 +403,8 @@
         ),
         name="block",
     )(
-        tokens, stale_kv, mods, jnp.swapaxes(spatial_qkv, 1, 2), spatial_out,
+        tokens, stale_kv, mod_table, mod_mix, timestep, frame_order,
+        jnp.asarray(angular_rates(width)), jnp.swapaxes(spatial_qkv, 1, 2), spatial_out,
         jnp.swapaxes(temporal_qkv, 1, 2), temporal_out,
     )
 

time: 217 us -> 213 us (0.982)
  other arithmetic: 3.14 us -> 0 us
where the time goes in v3:
time: 213 us
  Pallas kernels  211 us (99%)
    pallas_call x1, Pallas kernels, per_device(): pl.pallas_call(kernel, out_shape=pltpu.VMEM((rows, width), F32), in_specs...  211 us

profile of v3, /device:TPU:37, one launch (start us, length us, event | category | flops | bytes accessed | tf_op | source)
XLA Modules:
  0.0 212.7 jit_solution(5871968517265754004)
XLA Ops:
  0.7 210.6 %block.1 = f32[512,1152]{1,0:T(8,128)S(1)} custom-call(bf16[512,1152]{1,0:T(8,128)(2,1)} %tokens.1, bf16[512,1152]{1,0:T(8,128)(2,1)} %stale.1, f32[6,1152]{1,0:T(8,128)} %table_in.1, f32[6,1152]{1,0:T(8,128)} %mix_in.1, s32[1]{0:T(128)S(6)} %copy.14.time_in, s32[16]{0:T(128)} %order_in.1, f32[1,1152]{1,0:T(1,128)} %constant.2.clone.rates_in, ...), custom_call_target="tpu_custom_call" | custom-call | tf_op jit(solution)/shard_map/block/pallas_call | solution.py:363
  211.3 1.4 copy.13

commit v4 on v3

--- a/solution.py
+++ b/solution.py
@@ -104,10 +104,9 @@
         )
 
     barrier = pltpu.get_barrier_semaphore()
-    before, after_me = (frame + frames - 1) % frames, (frame + 1) % frames
-    near = [partner, opposite]
-    for j in (before, after_me):
-        near += [j * 4 + quarter, j * 4 + across]
+    chips, chip, core = devices // 2, me // 2, me % 2
+    before, after_me = (chip + chips - 1) % chips, (chip + 1) % chips
+    near = [partner, before * 2 + core, after_me * 2 + core]
     for device in near:
         pl.semaphore_signal(barrier, inc=1, device_id={"patch": device}, device_id_type=MESH)
 
@@ -119,17 +118,17 @@
     ]
     small = [pltpu.make_async_copy(a, b, small_sem.at[i]) for i, (a, b) in enumerate(small)]
     loads = [pltpu.make_async_copy(a, b, load_sem.at[i]) for i, (a, b) in enumerate(loads)]
-    for copy in loads[:1] + small + loads[1:]:
+    for copy in loads[:1] + small:
         copy.start()
     pl.semaphore_wait(barrier, len(near))
 
-    distances = [1 << n for n in range(frames.bit_length() - 2)]
+    distances = [1 << n for n in range(chips.bit_length() - 2)]
 
     def say(n):
-        for away in (distances[n], frames - distances[n]):
-            j = (frame + away) % frames
+        for away in (distances[n], chips - distances[n]):
+            there = (chip + away) % chips * 2 + core
             pl.semaphore_signal(
-                known.at[n], inc=1, device_id={"patch": j * 4 + quarter}, device_id_type=MESH
+                known.at[n], inc=1, device_id={"patch": there}, device_id_type=MESH
             )
 
     def hear(n):
@@ -140,6 +139,8 @@
         part = stale.at[pl.ds(lo, hi - lo), :]
         remote(part, kvb.at[2, pl.ds(lo, hi - lo), :], kv_send.at[0], kv_recv.at[n], opposite).start()
     remote(stale, kvb.at[1], kv_send.at[1], part_recv, partner).start()
+    for copy in loads[1:]:
+        copy.start()
 
     say(0)
 
@@ -178,9 +179,8 @@
         return c
 
     lax.fori_loop(0, rows // WINDOW, fresh, 0)
-    for n in range(1, len(distances) - 1):
-        hear(n)
-        say(n + 1)
+    hear(1)
+    say(2)
 
     whole = pl.ds(0, rows)
 
@@ -224,6 +224,9 @@
         acc[h, own, :] = acc[h, own, :] * wide(fade, WINDOW) + product
 
     each_head(lambda h: attend(h, [(0, whole)]))
+    for n in range(2, len(distances) - 1):
+        hear(n)
+        say(n + 1)
     remote(stale, kvb.at[1], kv_send.at[1], part_recv, partner).wait_recv()
     each_head(lambda h: attend(h, [(1, whole)]))
 
@@ -396,7 +399,7 @@
             pltpu.VMEM((TURNS, frames, piece * win // LANES, LANES), BF16),
             dma((5,)), dma((5,)), dma((3,)), dma((pieces,)), dma, dma((pieces,)),
             dma, dma((TURNS,)), dma, dma((TURNS,)),
-            pltpu.SemaphoreType.REGULAR((max(frames.bit_length() - 2, 1),)),
+            pltpu.SemaphoreType.REGULAR(((2 * frames).bit_length() - 2,)),
         ],
         compiler_params=pltpu.CompilerParams(
             collective_id=0, has_side_effects=True, vmem_limit_bytes=52 * 1024 * 1024

time: 213 us -> 212 us (level)
  no operation moved by 1% of the time
where the time goes in v4:
time: 212 us
  Pallas kernels  210 us (99%)
    pallas_call x1, Pallas kernels, per_device(): pl.pallas_call(kernel, out_shape=pltpu.VMEM((rows, width), F32), in_specs...  210 us

profile of v4, /device:TPU:37, one launch (start us, length us, event | category | flops | bytes accessed | tf_op | source)
XLA Modules:
  0.0 212.0 jit_solution(14622802817687679509)
XLA Ops:
  0.7 210.0 %block.1 = f32[512,1152]{1,0:T(8,128)S(1)} custom-call(bf16[512,1152]{1,0:T(8,128)(2,1)} %tokens.1, bf16[512,1152]{1,0:T(8,128)(2,1)} %stale.1, f32[6,1152]{1,0:T(8,128)} %table_in.1, f32[6,1152]{1,0:T(8,128)} %mix_in.1, s32[1]{0:T(128)S(6)} %copy.14.time_in, s32[16]{0:T(128)} %order_in.1, f32[1,1152]{1,0:T(1,128)} %constant.2.clone.rates_in, ...), custom_call_target="tpu_custom_call" | custom-call | tf_op jit(solution)/shard_map/block/pallas_call | solution.py:366
  210.6 1.4 copy.13
